TPU v7x, 32 devices: a whole 2x2x4 slice. The times are simulated.
32 devices in a mesh: seq: 8 (over z, x), fsdp: 4 (over y, core).
Axes of the slice: x: 2, y: 2, z: 4, core: 2. Of those that a mesh axis runs over, the one named last changes fastest.
Arguments:
- tokens: bfloat16 [4, 1024, 2048], P('fsdp', 'seq'), may hold values from -6 to 6
- cotangent: bfloat16 [4, 1024, 2048], P('fsdp', 'seq'), may hold values from -6 to 6
- routes: int32 [4, 1024, 8], P('fsdp', 'seq'), may hold values from 0 to 63, all different within a row; in each aligned block of 128 rows (0 to 127, 128 to 255, ..., all dimensions but the last counted through in order) at most 32 rows name the same one
- norm1_gain: bfloat16 [2048], P(('seq', 'fsdp')), may hold values from 0.099609375 to 1.8984375
- query_weight: bfloat16 [2048, 2048], P(('seq', 'fsdp')), may hold values from -0.125 to 0.125
- key_weight: bfloat16 [2048, 2048], P(('seq', 'fsdp')), may hold values from -0.125 to 0.125
- value_weight: bfloat16 [2048, 2048], P(('seq', 'fsdp')), may hold values from -0.125 to 0.125
- output_weight: bfloat16 [2048, 2048], P(('seq', 'fsdp')), may hold values from -2 to 2
- norm2_gain: bfloat16 [2048], P(('seq', 'fsdp')), may hold values from 0.099609375 to 1.8984375
- router_weight: bfloat16 [2048, 64], P(('seq', 'fsdp')), may hold values from -0.125 to 0.125
- expert_gate: bfloat16 [128, 2048, 512], P(('seq', 'fsdp')), may hold values from -0.125 to 0.125
- expert_up: bfloat16 [128, 2048, 512], P(('seq', 'fsdp')), may hold values from -0.125 to 0.125
- expert_down: bfloat16 [128, 512, 2048], P(('seq', 'fsdp')), may hold values from -0.75 to 0.75
Outputs:
- block_out: bfloat16 [4, 1024, 2048], P('fsdp', 'seq')
- input_grad: float32 [4, 1024, 2048], P('fsdp', 'seq')
- norm1_gain_grad: float32 [2048], P(('seq', 'fsdp'))
- query_weight_grad: float32 [2048, 2048], P(('seq', 'fsdp'))
- key_weight_grad: float32 [2048, 2048], P(('seq', 'fsdp'))
- value_weight_grad: float32 [2048, 2048], P(('seq', 'fsdp'))
- output_weight_grad: float32 [2048, 2048], P(('seq', 'fsdp'))
- norm2_gain_grad: float32 [2048], P(('seq', 'fsdp'))
- router_weight_grad: float32 [2048, 64], P(('seq', 'fsdp'))
- expert_gate_grad: float32 [128, 2048, 512], P(('seq', 'fsdp'))
- expert_up_grad: float32 [128, 2048, 512], P(('seq', 'fsdp'))
- expert_down_grad: float32 [128, 512, 2048], P(('seq', 'fsdp'))
Inputs may be any that keep to these rules, and one draw needn't show every extreme that they name: `routes`: each row names 8 different experts. Among the 128 rows of one device (aligned blocks of the flattened sequences) no expert is named more than 32 times, and in every draw some expert is named exactly 32 times in some block; every expert is named somewhere.
All inputs are finite; a program needn't handle non-finite values.
Results may differ from a plain program's by a relative error of at most 0.02.
Values may be sent and summed in bfloat16 or wider, within the bound.
A program may use at most 448 MiB of HBM per device.

v0:
```python
import jax
import jax.numpy as jnp
from jax import lax
from jax.sharding import PartitionSpec as P

H = 16
HD = 128
SPLIT = 2


epsilon = 1e-06
rope_base = 50000.0


def norm_rows(values, scales):
    mean_sq = jnp.mean(values * values, axis=-1, keepdims=True)
    return values * lax.rsqrt(mean_sq + epsilon) * scales


def rope_tables(positions, head_dim):
    half_dim = head_dim // 2
    frequency = rope_base ** (-(2.0 * jnp.arange(half_dim, dtype=jnp.float32)) / head_dim)
    angles = positions.astype(jnp.float32)[:, None] * frequency[None, :]
    return (jnp.cos(angles), jnp.sin(angles))


def rotate(values, cosine, sine_tab, inverse):
    half_dim = values.shape[-1] // 2
    low_half = values[..., :half_dim]
    high_half = values[..., half_dim:]
    cos_rows = cosine[:, None, :]
    sin_rows = sine_tab[:, None, :]
    if inverse:
        return jnp.concatenate(
            [
                low_half * cos_rows + high_half * sin_rows,
                high_half * cos_rows - low_half * sin_rows,
            ],
            axis=-1,
        )
    return jnp.concatenate(
        [low_half * cos_rows - high_half * sin_rows, high_half * cos_rows + low_half * sin_rows],
        axis=-1,
    )


def log_sum_exp(scores):
    return jnp.log(jnp.sum(jnp.exp(scores), axis=-1))


def route_weights(logits, chosen):
    expo = jnp.exp(logits)
    probability = expo / jnp.sum(expo, axis=-1, keepdims=True)
    picked = jnp.take_along_axis(probability, chosen, axis=-1)
    return picked / jnp.sum(picked, axis=-1, keepdims=True)


def gram_product(left, right):
    return lax.dot_general(
        left, right, (((0,), (0,)), ((), ())), preferred_element_type=jnp.float32
    )


def project_back(left, right):
    return lax.dot_general(
        left, right, (((1,), (1,)), ((), ())), preferred_element_type=jnp.float32
    )


def attend_heads(queries, keys_all, values_all):
    length, head_count, head_dim = queries.shape
    block_rows = min(512, length)
    score_scale = head_dim ** (-0.5)
    grouped = queries.reshape(length // block_rows, block_rows, head_count, head_dim)

    def one_block(query_block):
        scores = (
            jnp.einsum("qhd,khd->hqk", query_block, keys_all, preferred_element_type=jnp.float32)
            * score_scale
        )
        totals = log_sum_exp(scores)
        weights = jnp.exp(scores - totals[..., None]).astype(jnp.bfloat16)
        output = jnp.einsum("hqk,khd->qhd", weights, values_all, preferred_element_type=jnp.float32)
        return (output.astype(jnp.bfloat16), totals)

    outputs, totals = lax.map(one_block, grouped)
    return (outputs.reshape(length, head_count, head_dim), totals)


def attend_back(queries, keys_all, values_all, outputs, totals, grad_out):
    length, head_count, head_dim = queries.shape
    block_rows = min(512, length)
    count_blocks = length // block_rows
    score_scale = head_dim ** (-0.5)

    def to_blocks(array):
        return array.reshape(count_blocks, block_rows, head_count, head_dim)

    def one_block(running, inputs):
        key_sum, value_sum = running
        query_block, output_block, grad_block, total_block = inputs
        delta_rows = jnp.sum(
            grad_block.astype(jnp.float32) * output_block.astype(jnp.float32), axis=-1
        )
        scores = (
            jnp.einsum("qhd,khd->hqk", query_block, keys_all, preferred_element_type=jnp.float32)
            * score_scale
        )
        weights = jnp.exp(scores - total_block[..., None])
        value_sum = value_sum + jnp.einsum(
            "hqk,qhd->khd",
            weights.astype(jnp.bfloat16),
            grad_block,
            preferred_element_type=jnp.float32,
        )
        weight_grad = jnp.einsum(
            "qhd,khd->hqk", grad_block, values_all, preferred_element_type=jnp.float32
        )
        score_grad = (weights * (weight_grad - delta_rows.T[:, :, None]) * score_scale).astype(
            jnp.bfloat16
        )
        query_grad = jnp.einsum(
            "hqk,khd->qhd", score_grad, keys_all, preferred_element_type=jnp.float32
        ).astype(jnp.bfloat16)
        key_sum = key_sum + jnp.einsum(
            "hqk,qhd->khd", score_grad, query_block, preferred_element_type=jnp.float32
        )
        return ((key_sum, value_sum), query_grad)

    zeros_kv = jnp.zeros(keys_all.shape, jnp.float32)
    (key_sum, value_sum), query_grad = lax.scan(
        one_block,
        (zeros_kv, zeros_kv),
        (to_blocks(queries), to_blocks(outputs), to_blocks(grad_out), totals),
    )
    return (
        query_grad.reshape(length, head_count, head_dim),
        key_sum.astype(jnp.bfloat16),
        value_sum.astype(jnp.bfloat16),
    )


def to_experts(rows, experts, capacity):
    model_width = rows.shape[1]
    seq_count = lax.axis_size("seq")
    fsdp_count = lax.axis_size("fsdp")
    devices = seq_count * fsdp_count
    per_device = experts * SPLIT // devices
    spread = jnp.broadcast_to(
        rows.reshape(experts, 1, capacity, model_width), (experts, SPLIT, capacity, model_width)
    )
    moved = lax.all_to_all(
        spread.reshape(devices, per_device, capacity, model_width),
        ("seq", "fsdp"),
        split_axis=0,
        concat_axis=0,
        tiled=True,
    )
    return moved


def from_experts(parts):
    devices, per_device, capacity, model_width = parts.shape
    moved = lax.all_to_all(parts, ("seq", "fsdp"), split_axis=0, concat_axis=0, tiled=True)
    halves = moved.reshape(devices * per_device // SPLIT, SPLIT, capacity, model_width)
    summed = halves[:, 0].astype(jnp.float32)
    summed = summed + halves[:, 1].astype(jnp.float32)
    return summed.reshape(-1, model_width)


def body(
    tokens,
    cotangent,
    routes,
    norm1_gain,
    query_weight,
    key_weight,
    value_weight,
    output_weight,
    norm2_gain,
    router_weight,
    expert_gate,
    expert_up,
    expert_down,
):
    shards = (
        query_weight,
        key_weight,
        value_weight,
        output_weight,
        router_weight,
        norm1_gain,
        norm2_gain,
    )
    query_full, key_full, value_full, output_full, router_full, first_gain, second_gain = (
        lax.all_gather(shards[0], ("seq", "fsdp"), axis=0, tiled=True),
        lax.all_gather(shards[1], ("seq", "fsdp"), axis=0, tiled=True),
        lax.all_gather(shards[2], ("seq", "fsdp"), axis=0, tiled=True),
        lax.all_gather(shards[3], ("seq", "fsdp"), axis=0, tiled=True),
        lax.all_gather(shards[4], ("seq", "fsdp"), axis=0, tiled=True),
        lax.all_gather(shards[5], ("seq", "fsdp"), axis=0, tiled=True),
        lax.all_gather(shards[6], ("seq", "fsdp"), axis=0, tiled=True),
    )
    tok_rows = tokens.shape[1]
    model_width = tokens.shape[2]
    inputs_x = tokens[0]
    positions = lax.axis_index("seq") * tok_rows + jnp.arange(tok_rows, dtype=jnp.int32)
    cosine, sine_tab = rope_tables(positions, HD)
    gain_in = first_gain.astype(jnp.float32)
    gain_mid = second_gain.astype(jnp.float32)
    normed_in = norm_rows(inputs_x.astype(jnp.float32), gain_in).astype(jnp.bfloat16)
    query_rot = rotate(
        jnp.dot(normed_in, query_full, preferred_element_type=jnp.float32).reshape(tok_rows, H, HD),
        cosine,
        sine_tab,
        False,
    ).astype(jnp.bfloat16)
    key_rot = rotate(
        jnp.dot(normed_in, key_full, preferred_element_type=jnp.float32).reshape(tok_rows, H, HD),
        cosine,
        sine_tab,
        False,
    ).astype(jnp.bfloat16)
    value_rows = (
        jnp.dot(normed_in, value_full, preferred_element_type=jnp.float32)
        .astype(jnp.bfloat16)
        .reshape(tok_rows, H, HD)
    )
    query_heads, key_heads, value_heads = (
        lax.all_to_all(query_rot, "seq", split_axis=1, concat_axis=0, tiled=True),
        lax.all_to_all(key_rot, "seq", split_axis=1, concat_axis=0, tiled=True),
        lax.all_to_all(value_rows, "seq", split_axis=1, concat_axis=0, tiled=True),
    )
    attn_heads, totals = attend_heads(query_heads, key_heads, value_heads)
    attn_rows = lax.all_to_all(attn_heads, "seq", split_axis=0, concat_axis=1, tiled=True).reshape(
        tok_rows, model_width
    )
    residual = inputs_x.astype(jnp.float32) + jnp.dot(
        attn_rows, output_full, preferred_element_type=jnp.float32
    )
    normed_mid = norm_rows(residual, gain_mid).astype(jnp.bfloat16)
    logits = jnp.dot(normed_mid, router_full, preferred_element_type=jnp.float32)
    chosen = routes[0]
    weights = route_weights(logits, chosen)
    experts = router_full.shape[1]
    top_k = chosen.shape[1]
    capacity = tok_rows * top_k // experts * 2
    flat_routes = chosen.reshape(-1)
    onehot = (flat_routes[:, None] == jnp.arange(experts, dtype=jnp.int32)[None, :]).astype(
        jnp.int32
    )
    before = jnp.cumsum(onehot, axis=0) - onehot
    slot_pos = jnp.sum(before * onehot, axis=1)
    target = flat_routes * capacity + slot_pos
    send_rows = (
        jnp.zeros((experts * capacity, model_width), jnp.bfloat16)
        .at[target]
        .set(jnp.repeat(normed_mid, top_k, axis=0))
    )
    received = to_experts(send_rows, experts, capacity)
    pre_gate = jnp.einsum(
        "spcd,pdf->spcf", received, expert_gate, preferred_element_type=jnp.float32
    )
    pre_up = jnp.einsum("spcd,pdf->spcf", received, expert_up, preferred_element_type=jnp.float32)
    gate_sigmoid = jax.nn.sigmoid(pre_gate)
    active = pre_gate * gate_sigmoid
    hidden = (active * pre_up).astype(jnp.bfloat16)
    piece_out = jnp.einsum(
        "spcf,pfd->spcd", hidden, expert_down, preferred_element_type=jnp.float32
    ).astype(jnp.bfloat16)
    expert_rows = from_experts(piece_out)[target].reshape(tok_rows, top_k, model_width)
    moe = jnp.sum(weights[:, :, None] * expert_rows, axis=1)
    block_out = (residual + moe).astype(jnp.bfloat16)
    cot = cotangent[0].astype(jnp.float32)
    weight_grad = jnp.sum(cot[:, None, :] * expert_rows, axis=-1)
    routed_grad = (
        (weights[:, :, None] * cot[:, None, :])
        .astype(jnp.bfloat16)
        .reshape(tok_rows * top_k, model_width)
    )
    send_grad = (
        jnp.zeros((experts * capacity, model_width), jnp.bfloat16).at[target].set(routed_grad)
    )
    received_grad = to_experts(send_grad, experts, capacity)
    hidden_grad = jnp.einsum(
        "spcd,pfd->spcf", received_grad, expert_down, preferred_element_type=jnp.float32
    )
    down_grad = jnp.einsum(
        "spcf,spcd->pfd", hidden, received_grad, preferred_element_type=jnp.float32
    )
    gate_grad = (
        hidden_grad * pre_up * gate_sigmoid * (1.0 + pre_gate * (1.0 - gate_sigmoid))
    ).astype(jnp.bfloat16)
    up_grad = (hidden_grad * active).astype(jnp.bfloat16)
    gate_weight_grad = jnp.einsum(
        "spcd,spcf->pdf", received, gate_grad, preferred_element_type=jnp.float32
    )
    up_weight_grad = jnp.einsum(
        "spcd,spcf->pdf", received, up_grad, preferred_element_type=jnp.float32
    )
    piece_back = (
        jnp.einsum("spcf,pdf->spcd", gate_grad, expert_gate, preferred_element_type=jnp.float32)
        + jnp.einsum("spcf,pdf->spcd", up_grad, expert_up, preferred_element_type=jnp.float32)
    ).astype(jnp.bfloat16)
    moe_in_grad = jnp.sum(
        from_experts(piece_back)[target].reshape(tok_rows, top_k, model_width), axis=1
    )
    query_back, key_back, value_back, output_back, router_back, first_back, second_back = (
        lax.all_gather(shards[0], ("seq", "fsdp"), axis=0, tiled=True),
        lax.all_gather(shards[1], ("seq", "fsdp"), axis=0, tiled=True),
        lax.all_gather(shards[2], ("seq", "fsdp"), axis=0, tiled=True),
        lax.all_gather(shards[3], ("seq", "fsdp"), axis=0, tiled=True),
        lax.all_gather(shards[4], ("seq", "fsdp"), axis=0, tiled=True),
        lax.all_gather(shards[5], ("seq", "fsdp"), axis=0, tiled=True),
        lax.all_gather(shards[6], ("seq", "fsdp"), axis=0, tiled=True),
    )
    _, route_back = jax.vjp(lambda values: route_weights(values, chosen), logits)
    logit_grad = route_back(weight_grad)[0].astype(jnp.bfloat16)
    normed_total = moe_in_grad + project_back(logit_grad, router_back)
    grad_router = gram_product(normed_mid, logit_grad)
    _, norm_back = jax.vjp(norm_rows, residual, second_back.astype(jnp.float32))
    resid_part, grad_gain_two = norm_back(normed_total)
    resid_grad = cot + resid_part
    resid_round = resid_grad.astype(jnp.bfloat16)
    attn_grad = project_back(resid_round, output_back).astype(jnp.bfloat16).reshape(tok_rows, H, HD)
    attn_grad_heads = lax.all_to_all(attn_grad, "seq", split_axis=1, concat_axis=0, tiled=True)
    query_grad, key_grad, value_grad = attend_back(
        query_heads, key_heads, value_heads, attn_heads, totals, attn_grad_heads
    )
    seq_positions = jnp.arange(query_grad.shape[0], dtype=jnp.int32)
    cosine_all, sine_all = rope_tables(seq_positions, HD)
    query_head_rows = rotate(query_grad.astype(jnp.float32), cosine_all, sine_all, True).astype(
        jnp.bfloat16
    )
    key_head_rows = rotate(key_grad.astype(jnp.float32), cosine_all, sine_all, True).astype(
        jnp.bfloat16
    )
    query_back_rows, key_back_rows, value_back_rows = (
        lax.all_to_all(query_head_rows, "seq", split_axis=0, concat_axis=1, tiled=True),
        lax.all_to_all(key_head_rows, "seq", split_axis=0, concat_axis=1, tiled=True),
        lax.all_to_all(value_grad, "seq", split_axis=0, concat_axis=1, tiled=True),
    )
    query_rows = query_back_rows.reshape(tok_rows, model_width)
    key_rows = key_back_rows.reshape(tok_rows, model_width)
    value_grad_rows = value_back_rows.reshape(tok_rows, model_width)
    normed_in_grad = (
        project_back(query_rows, query_back)
        + project_back(key_rows, key_back)
        + project_back(value_grad_rows, value_back)
    )
    _, norm_back_in = jax.vjp(
        norm_rows, inputs_x.astype(jnp.float32), first_back.astype(jnp.float32)
    )
    input_part, grad_gain_one = norm_back_in(normed_in_grad)
    input_grad = resid_grad + input_part
    grad_output = gram_product(attn_rows, resid_round)
    grad_query = gram_product(normed_in, query_rows)
    grad_key = gram_product(normed_in, key_rows)
    grad_value = gram_product(normed_in, value_grad_rows)
    summed = (
        lax.psum_scatter(grad_query, ("seq", "fsdp"), scatter_dimension=0, tiled=True),
        lax.psum_scatter(grad_key, ("seq", "fsdp"), scatter_dimension=0, tiled=True),
        lax.psum_scatter(grad_value, ("seq", "fsdp"), scatter_dimension=0, tiled=True),
        lax.psum_scatter(grad_output, ("seq", "fsdp"), scatter_dimension=0, tiled=True),
        lax.psum_scatter(grad_router, ("seq", "fsdp"), scatter_dimension=0, tiled=True),
        lax.psum_scatter(grad_gain_one, ("seq", "fsdp"), scatter_dimension=0, tiled=True),
        lax.psum_scatter(grad_gain_two, ("seq", "fsdp"), scatter_dimension=0, tiled=True),
    )
    final_query, final_key, final_value, final_output = (summed[0], summed[1], summed[2], summed[3])
    final_router, final_gain_one, final_gain_two = (summed[4], summed[5], summed[6])
    return (
        block_out[None],
        input_grad[None],
        final_gain_one,
        final_query,
        final_key,
        final_value,
        final_output,
        final_gain_two,
        final_router,
        gate_weight_grad,
        up_weight_grad,
        down_grad,
    )


def solution(mesh):
    placed = (
        P("fsdp", "seq", None),
        P("fsdp", "seq", None),
        P("fsdp", "seq", None),
        P(("seq", "fsdp")),
        P(("seq", "fsdp"), None),
        P(("seq", "fsdp"), None),
        P(("seq", "fsdp"), None),
        P(("seq", "fsdp"), None),
        P(("seq", "fsdp")),
        P(("seq", "fsdp"), None),
        P(("seq", "fsdp"), None, None),
        P(("seq", "fsdp"), None, None),
        P(("seq", "fsdp"), None, None),
    )
    return jax.shard_map(
        body,
        mesh=mesh,
        in_specs=placed,
        out_specs=(
            P("fsdp", "seq", None),
            P("fsdp", "seq", None),
            P(("seq", "fsdp")),
            P(("seq", "fsdp"), None),
            P(("seq", "fsdp"), None),
            P(("seq", "fsdp"), None),
            P(("seq", "fsdp"), None),
            P(("seq", "fsdp")),
            P(("seq", "fsdp"), None),
            P(("seq", "fsdp"), None, None),
            P(("seq", "fsdp"), None, None),
            P(("seq", "fsdp"), None, None),
        ),
        check_vma=False,
    )
```

profile of v0, /device:TPU:0, one launch (start us, length us, event | category | flops | bytes accessed | tf_op | source)
XLA Modules:
  0.0 2947.6 jit_solution(3488503030299215115)
XLA Ops:
  11.7 43.0 %all-reduce.5 = (bf16[2048]{0:T(1024)(128)(2,1)S(1)}, bf16[2048]{0:T(1024)(128)(2,1)S(1)}) all-reduce(bf16[2048]{0:T(1024)(128)(2,1)S(1)} %dynamic-update-slice, bf16[2048]{0:T(1024)(128)(2,1)S(1)} %dynamic-update-slice.1), channel_id=1, replica_groups=mesh['seq'=8,'fsdp'=4] {'seq','fsdp'}, use_global_device_ids=true, to_apply=%add | all-reduce | flops 4096 | bytes 16384
  56.2 34.6 %all-gather.7.cloned.1.call-done = bf16[2048,2048]{1,0:T(8,128)(2,1)} async-done(((bf16[64,2048]{1,0:T(8,128)(2,1)}), bf16[2048,2048]{1,0:T(8,128)(2,1)}) %all-gather.7.cloned.1.call-update) | async-done | bytes 8388624 | tf_op jit(solution)/shard_map/all_gather | solution.py:197
  103.1 66.3 %all-gather.5.cloned.1.call-done = bf16[2048,2048]{1,0:T(8,128)(2,1)} async-done(((bf16[64,2048]{1,0:T(8,128)(2,1)}), bf16[2048,2048]{1,0:T(8,128)(2,1)}) %all-gather.5.cloned.1.call-update) | async-done | bytes 8388624 | tf_op jit(solution)/shard_map/all_gather | solution.py:196
  196.3 25.1 all-to-all-done.1
  225.2 39.3 %all-gather.9.cloned.1.call-done = bf16[2048,2048]{1,0:T(8,128)(2,1)} async-done(((bf16[64,2048]{1,0:T(8,128)(2,1)}), bf16[2048,2048]{1,0:T(8,128)(2,1)}) %all-gather.9.cloned.1.call-update) | async-done | bytes 8388624 | tf_op jit(solution)/shard_map/all_gather | solution.py:198
  274.9 19.7 all-to-all-done.2
  306.2 18.0 reduce-window.6
  327.3 25.9 all-gather.11.cloned.1.call-done
  386.4 337.4 %all_gather.34 = bf16[2048,64]{1,0:T(8,128)(2,1)S(1)} all-gather(bf16[64,64]{1,0:T(8,128)(2,1)S(1)} %copy-done.50), channel_id=1, replica_groups=mesh['seq'=8,'fsdp'=4] {'seq','fsdp'}, dimensions={0}, use_global_device_ids=true | all-gather | bytes 270336 | tf_op jit(solution)/shard_map/all_gather | solution.py:200
  762.4 59.2 %all-to-all-start.6 = ((bf16[32,4,32,2048]{3,2,1,0:T(8,128)(2,1)}), bf16[32,4,32,2048]{3,2,1,0:T(8,128)(2,1)}, u32[]{:S(2)}, u32[]{:S(2)}) async-start(bf16[32,4,32,2048]{3,2,1,0:T(8,128)(2,1)} %bitcast.380), calls=%async_computation.6 | async-start | bytes 33554432 | tf_op jit(solution)/shard_map/all_to_all | solution.py:152
  855.2 332.0 %all-to-all-done.6 = bf16[32,4,32,2048]{3,2,1,0:T(8,128)(2,1)} async-done(((bf16[32,4,32,2048]{3,2,1,0:T(8,128)(2,1)}), bf16[32,4,32,2048]{3,2,1,0:T(8,128)(2,1)}, u32[]{:S(2)}, u32[]{:S(2)}) %all-to-all-start.6) | async-done | bytes 16777248 | tf_op jit(solution)/shard_map/all_to_all | solution.py:152
  1187.2 22.8 fusion.57
  1257.3 18.7 fusion.51
  1276.1 22.3 fusion.48
  1312.6 310.3 %all-to-all-done.5 = bf16[32,4,32,2048]{3,2,1,0:T(8,128)(2,1)} async-done(((bf16[32,4,32,2048]{3,2,1,0:T(8,128)(2,1)}), bf16[32,4,32,2048]{3,2,1,0:T(8,128)(2,1)}, u32[]{:S(2)}, u32[]{:S(2)}) %all-to-all-start.5) | async-done | bytes 16777248 | tf_op jit(solution)/shard_map/all_to_all | solution.py:164
  1680.1 324.9 %all-to-all-done.7 = bf16[32,4,32,2048]{3,2,1,0:T(8,128)(2,1)} async-done(((bf16[32,4,32,2048]{3,2,1,0:T(8,128)(2,1)}), bf16[32,4,32,2048]{3,2,1,0:T(8,128)(2,1)}, u32[]{:S(2)}, u32[]{:S(2)}) %all-to-all-start.7) | async-done | bytes 16777248 | tf_op jit(solution)/shard_map/all_to_all | solution.py:164
  2083.1 23.7 while.28
  2112.4 18.3 all_to_all.146
  2140.2 17.8 all_to_all.147
  2262.7 54.8 %all-reduce.4 = (f32[2048]{0:T(1024)S(1)}, f32[2048]{0:T(1024)S(1)}) all-reduce(f32[2048]{0:T(1024)S(1)} %get-tuple-element.205, f32[2048]{0:T(1024)S(1)} %copy-done.49), channel_id=2, replica_groups=mesh['seq'=8,'fsdp'=4] {'seq','fsdp'}, use_global_device_ids=true, to_apply=%region_24.25.clone | all-reduce | flops 4096 | bytes 32768
  2320.0 56.6 %reduce-scatter.12.cloned.1.call-done = f32[64,2048]{1,0:T(8,128)} async-done(((f32[2048,2048]{1,0:T(8,128)}), f32[64,2048]{1,0:T(8,128)}) %reduce-scatter.12.cloned.1.call-update) | async-done | bytes 524304 | tf_op jit(solution)/shard_map/reduce_scatter | solution.py:364
  2376.6 187.3 %reduce-scatter.8.cloned.1.call-done = f32[64,2048]{1,0:T(8,128)} async-done(((f32[2048,2048]{1,0:T(8,128)}), f32[64,2048]{1,0:T(8,128)}) %reduce-scatter.8.cloned.1.call-update) | async-done | bytes 524304 | tf_op jit(solution)/shard_map/reduce_scatter | solution.py:362
  2563.9 188.4 %reduce-scatter.6.cloned.1.call-done = f32[64,2048]{1,0:T(8,128)} async-done(((f32[2048,2048]{1,0:T(8,128)}), f32[64,2048]{1,0:T(8,128)}) %reduce-scatter.6.cloned.1.call-update) | async-done | bytes 524304 | tf_op jit(solution)/shard_map/reduce_scatter | solution.py:361
  2752.3 188.3 %reduce-scatter.10.cloned.1.call-done = f32[64,2048]{1,0:T(8,128)} async-done(((f32[2048,2048]{1,0:T(8,128)}), f32[64,2048]{1,0:T(8,128)}) %reduce-scatter.10.cloned.1.call-update) | async-done | bytes 524304 | tf_op jit(solution)/shard_map/reduce_scatter | solution.py:363
  (332 shorter events, 525.6 us)
Async XLA Ops:
  7.2 83.7 %all-gather.7.cloned.1.call-start = ((), (), s32[]{:S(2)}) async-start(), calls=%async_computation.18 | async-start | bytes 8650752 | tf_op jit(solution)/shard_map/all_gather | solution.py:197
  7.9 161.5 %all-gather.5.cloned.1.call-start = ((), (), s32[]{:S(2)}) async-start(), calls=%async_computation.17 | async-start | bytes 8650752 | tf_op jit(solution)/shard_map/all_gather | solution.py:196
  8.7 255.9 %all-gather.9.cloned.1.call-start = ((), (), s32[]{:S(2)}) async-start(), calls=%async_computation.19 | async-start | bytes 8650752 | tf_op jit(solution)/shard_map/all_gather | solution.py:198
  9.4 343.8 %all-gather.11.cloned.1.call-start = ((), (), s32[]{:S(2)}) async-start(), calls=%async_computation.20 | async-start | bytes 8650752 | tf_op jit(solution)/shard_map/all_gather | solution.py:199
  191.4 30.0 %all-to-all-start.1 = ((bf16[128,16,128]{0,2,1:T(8,128)(2,1)}), bf16[128,16,128]{0,2,1:T(8,128)(2,1)S(1)}, u32[]{:S(2)}, u32[]{:S(2)}) async-start(bf16[128,16,128]{0,2,1:T(8,128)(2,1)} %pad_maximum_fusion.1), calls=%async_computation.1 | async-start | bytes 1048576 | tf_op jit(solution)/shard_map/all_to_all | solution.py:231
  221.4 48.8 %all-to-all-start = ((bf16[128,16,128]{0,2,1:T(8,128)(2,1)}), bf16[128,16,128]{0,2,1:T(8,128)(2,1)S(1)}, u32[]{:S(2)}, u32[]{:S(2)}) async-start(bf16[128,16,128]{0,2,1:T(8,128)(2,1)} %pad_maximum_fusion), calls=%async_computation | async-start | bytes 1048576 | tf_op jit(solution)/shard_map/all_to_all | solution.py:230
  270.2 24.4 all-to-all-start.2
  274.2 457.6 %copy-start.29 = (s32[1,128,8]{2,1,0:T(8,128)}, s32[1,128,8]{2,1,0:T(8,128)S(1)}, u32[]{:S(2)}) copy-start(s32[1,128,8]{2,1,0:T(8,128)S(1)} %copy.153) | copy-start | bytes 12292
  302.4 22.6 all-to-all-start.3
  325.1 407.6 %copy-start.51 = (s32[1024,1]{0,1:T(1,128)}, s32[1024,1]{0,1:T(1,128)S(1)}, u32[]{:S(2)}) copy-start(s32[1024,1]{0,1:T(1,128)S(1)} %compare_select_fusion.1) | copy-start | bytes 12292
  359.1 364.8 %copy-start.17 = (bf16[128,2048]{1,0:T(8,128)(2,1)}, bf16[128,2048]{1,0:T(8,128)(2,1)S(1)}, u32[]{:S(2)}) copy-start(bf16[128,2048]{1,0:T(8,128)(2,1)S(1)} %multiply_convert_fusion.1) | copy-start | bytes 1572868
  381.5 342.3 %copy-start.31 = (bf16[1,128,2048]{2,1,0:T(8,128)(2,1)S(1)}, bf16[1,128,2048]{2,1,0:T(8,128)(2,1)}, u32[]{:S(2)}) copy-start(bf16[1,128,2048]{2,1,0:T(8,128)(2,1)} %param.18) | copy-start | bytes 1572868
  381.6 370.0 %all-to-all-start.4 = ((bf16[32,4,32,2048]{3,2,1,0:T(8,128)(2,1)}), bf16[32,4,32,2048]{3,2,1,0:T(8,128)(2,1)}, u32[]{:S(2)}, u32[]{:S(2)}) async-start(bf16[32,4,32,2048]{3,2,1,0:T(8,128)(2,1)} %bitcast.379), calls=%async_computation.4 | async-start | bytes 33554432 | tf_op jit(solution)/shard_map/all_to_all | solution.py:152
  762.4 424.8 %all-to-all-start.6 = ((bf16[32,4,32,2048]{3,2,1,0:T(8,128)(2,1)}), bf16[32,4,32,2048]{3,2,1,0:T(8,128)(2,1)}, u32[]{:S(2)}, u32[]{:S(2)}) async-start(bf16[32,4,32,2048]{3,2,1,0:T(8,128)(2,1)} %bitcast.380), calls=%async_computation.6 | async-start | bytes 33554432 | tf_op jit(solution)/shard_map/all_to_all | solution.py:152
  1240.8 382.1 %all-to-all-start.5 = ((bf16[32,4,32,2048]{3,2,1,0:T(8,128)(2,1)}), bf16[32,4,32,2048]{3,2,1,0:T(8,128)(2,1)}, u32[]{:S(2)}, u32[]{:S(2)}) async-start(bf16[32,4,32,2048]{3,2,1,0:T(8,128)(2,1)} %copy.162), calls=%async_computation.5 | async-start | bytes 33554432 | tf_op jit(solution)/shard_map/all_to_all | solution.py:164
  1312.6 327.4 %copy-start.30 = (s32[1,128,8]{2,1,0:T(8,128)S(1)}, s32[1,128,8]{2,1,0:T(8,128)}, u32[]{:S(2)}) copy-start(s32[1,128,8]{2,1,0:T(8,128)} %copy-done.29) | copy-start | bytes 12292
  1312.6 327.4 %copy-start.37 = (f32[128,8]{1,0:T(8,128)S(1)}, f32[128,8]{1,0:T(8,128)}, u32[]{:S(2)}) copy-start(f32[128,8]{1,0:T(8,128)} %copy-done.36) | copy-start | bytes 12292
  1622.9 382.1 %all-to-all-start.7 = ((bf16[32,4,32,2048]{3,2,1,0:T(8,128)(2,1)}), bf16[32,4,32,2048]{3,2,1,0:T(8,128)(2,1)}, u32[]{:S(2)}, u32[]{:S(2)}) async-start(bf16[32,4,32,2048]{3,2,1,0:T(8,128)(2,1)} %copy.164), calls=%async_computation.7 | async-start | bytes 33554432 | tf_op jit(solution)/shard_map/all_to_all | solution.py:164
  1639.4 680.5 %reduce-scatter.14.cloned.1.call-start = ((), (), s32[]{:S(2)}) async-start(), calls=%async_computation.25 | async-start | bytes 1081344 | tf_op jit(solution)/shard_map/reduce_scatter | solution.py:365
  2043.3 333.3 %reduce-scatter.12.cloned.1.call-start = ((), (), s32[]{:S(2)}) async-start(), calls=%async_computation.24 | async-start | bytes 17301504 | tf_op jit(solution)/shard_map/reduce_scatter | solution.py:364
  2061.9 20.3 all-to-all-start.8
  2067.4 496.5 %reduce-scatter.8.cloned.1.call-start = ((), (), s32[]{:S(2)}) async-start(), calls=%async_computation.22 | async-start | bytes 17301504 | tf_op jit(solution)/shard_map/reduce_scatter | solution.py:362
  2139.3 613.0 %reduce-scatter.6.cloned.1.call-start = ((), (), s32[]{:S(2)}) async-start(), calls=%async_computation.21 | async-start | bytes 17301504 | tf_op jit(solution)/shard_map/reduce_scatter | solution.py:361
  2166.7 773.9 %reduce-scatter.10.cloned.1.call-start = ((), (), s32[]{:S(2)}) async-start(), calls=%async_computation.23 | async-start | bytes 17301504 | tf_op jit(solution)/shard_map/reduce_scatter | solution.py:363
  (65 other events, 3448.1 us)
Sparse Core Ops, SparseCore 0:
  10.8 79.9 all-gather.6
  93.7 75.6 all-gather.4
  172.3 92.1 all-gather.8
  267.3 85.8 all-gather.10
  2043.5 149.6 reduce-scatter.13
  2195.9 180.6 reduce-scatter.11
  2379.5 184.4 reduce-scatter.7
  2566.8 185.4 reduce-scatter.5
  2755.2 185.3 reduce-scatter.9
where the time goes:
time: 2960 us; the launch traced here: 2950 us
  waiting for transfers between devices  1820 us (61%)
  blocking collectives  488 us (16%)
  matrix products  269 us (9%)
  local copies, waits for them, and re-layouts  143 us (5%)
  starting transfers between devices  118 us (4%)
  other arithmetic  93.1 us (3%)
    all_to_all x2, waiting for transfers between devices, from_experts(): lax.all_to_all(parts, ('seq', 'fsdp'), split_axis=0, concat_axis=0, tiled...  635 us
    all_to_all x2, waiting for transfers between devices, to_experts(): lax.all_to_all(spread.reshape(devices, per_device, capacity, model_width)...  339 us
    all_gather x1, blocking collectives, body(): lax.all_gather(shards[4], ('seq', 'fsdp'), axis=0, tiled=True)  337 us
    reduce_scatter x1, waiting for transfers between devices, body(): lax.psum_scatter(grad_query, ('seq', 'fsdp'), scatter_dimension=0, tiled=...  188 us
    reduce_scatter x1, waiting for transfers between devices, body(): lax.psum_scatter(grad_value, ('seq', 'fsdp'), scatter_dimension=0, tiled=...  188 us
    reduce_scatter x1, waiting for transfers between devices, body(): lax.psum_scatter(grad_key, ('seq', 'fsdp'), scatter_dimension=0, tiled=True)  187 us
    unnamed x2, blocking collectives  97.8 us
    all_gather x1, waiting for transfers between devices, body(): lax.all_gather(shards[0], ('seq', 'fsdp'), axis=0, tiled=True)  66.3 us
  transfers between devices with their start and end apart: 18, of which 15 were waited for; matrix products, arithmetic and copies ran while one was open for 13% of the time, Pallas kernels for 0%

commit v1 on v0

v1 whole, which is shorter than its diff:
```python
import jax
import jax.numpy as jnp
from jax import lax
from jax.sharding import PartitionSpec as P

H = 16
HD = 128
SPLIT = 2
AXES = ("seq", "fsdp")

epsilon = 1e-06
rope_base = 50000.0
bf16 = jnp.bfloat16
f32 = jnp.float32


def norm_rows(values, scales):
    mean_sq = jnp.mean(values * values, axis=-1, keepdims=True)
    return values * lax.rsqrt(mean_sq + epsilon) * scales


def rope_tables(positions, head_dim):
    half_dim = head_dim // 2
    frequency = rope_base ** (-(2.0 * jnp.arange(half_dim, dtype=f32)) / head_dim)
    angles = positions.astype(f32)[:, None] * frequency[None, :]
    return (jnp.cos(angles), jnp.sin(angles))


def rotate(values, cosine, sine_tab, inverse):
    half_dim = values.shape[-1] // 2
    low_half = values[..., :half_dim]
    high_half = values[..., half_dim:]
    cos_rows = cosine[:, None, :]
    sin_rows = -sine_tab[:, None, :] if inverse else sine_tab[:, None, :]
    return jnp.concatenate(
        [low_half * cos_rows - high_half * sin_rows, high_half * cos_rows + low_half * sin_rows],
        axis=-1,
    )


def route_weights(logits, chosen):
    expo = jnp.exp(logits)
    probability = expo / jnp.sum(expo, axis=-1, keepdims=True)
    experts = jnp.arange(logits.shape[1], dtype=jnp.int32)
    match = (chosen[:, :, None] == experts).astype(f32)
    picked = jnp.sum(match * probability[:, None, :], axis=-1)
    return picked / jnp.sum(picked, axis=-1, keepdims=True)


def mm(left, right):
    return jnp.dot(left, right, preferred_element_type=f32)


def mm_tn(left, right):
    return lax.dot_general(left, right, (((0,), (0,)), ((), ())), preferred_element_type=f32)


def mm_nt(left, right):
    return lax.dot_general(left, right, (((1,), (1,)), ((), ())), preferred_element_type=f32)


def ein(spec, *args):
    return jnp.einsum(spec, *args, preferred_element_type=f32)


def body(
    tokens,
    cotangent,
    routes,
    norm1_gain,
    query_weight,
    key_weight,
    value_weight,
    output_weight,
    norm2_gain,
    router_weight,
    expert_gate,
    expert_up,
    expert_down,
):
    n_seq = lax.axis_size("seq")
    n_fsdp = lax.axis_size("fsdp")
    n_dev = n_seq * n_fsdp
    seq_at = lax.axis_index("seq")
    dev_at = seq_at * n_fsdp + lax.axis_index("fsdp")
    tok_rows, width = tokens.shape[1], tokens.shape[2]
    length = tok_rows * n_seq
    heads = H // n_seq
    cols = heads * HD
    shard = query_weight.shape[0]
    experts = router_weight.shape[1]
    top_k = routes.shape[2]
    capacity = tok_rows * top_k // experts * 2
    pieces = expert_gate.shape[0]
    n_loc = max(1, pieces // SPLIT)
    per_loc = pieces // n_loc
    first_expert = dev_at * pieces // SPLIT

    x_own = tokens[0]
    cot_own = cotangent[0]
    chosen = routes[0]

    routes_all = lax.all_gather(chosen, AXES, axis=0, tiled=True)
    x_seq = lax.all_gather(x_own, "seq", axis=0, tiled=True)
    small = jnp.concatenate(
        [
            router_weight,
            norm1_gain[:, None],
            norm2_gain[:, None],
            jnp.zeros((shard, 128 - experts - 2), bf16),
        ],
        axis=1,
    )
    blocks = jnp.concatenate(
        [
            query_weight.reshape(shard, n_seq, cols),
            key_weight.reshape(shard, n_seq, cols),
            value_weight.reshape(shard, n_seq, cols),
            jnp.broadcast_to(small[:, None, :], (shard, n_seq, 128)),
        ],
        axis=2,
    ).transpose(1, 0, 2)
    moved = lax.all_to_all(blocks, "seq", split_axis=0, concat_axis=0, tiled=True)
    packed = lax.all_gather(moved, "fsdp", axis=1).reshape(width, 3 * cols + 128)
    w_qkv = packed[:, : 3 * cols]
    router_full = packed[:, 3 * cols : 3 * cols + experts]
    gain_in = packed[:, 3 * cols + experts].astype(f32)
    gain_mid = packed[:, 3 * cols + experts + 1].astype(f32)
    out_full = lax.all_gather(output_weight, AXES, axis=0, tiled=True)
    out_rows = lax.dynamic_slice_in_dim(out_full, seq_at * cols, cols, 0)
    cot_all = lax.all_gather(cot_own, AXES, axis=0, tiled=True)

    cosine, sine_tab = rope_tables(jnp.arange(length, dtype=jnp.int32), HD)
    normed_in = norm_rows(x_seq.astype(f32), gain_in).astype(bf16)
    qkv = mm(normed_in, w_qkv)
    q = rotate(qkv[:, :cols].reshape(length, heads, HD), cosine, sine_tab, False).astype(bf16)
    k = rotate(qkv[:, cols : 2 * cols].reshape(length, heads, HD), cosine, sine_tab, False).astype(bf16)
    v = qkv[:, 2 * cols :].astype(bf16).reshape(length, heads, HD)
    scale = HD ** (-0.5)
    scores = ein("qhd,khd->hqk", q, k) * scale
    totals = jnp.log(jnp.sum(jnp.exp(scores), axis=-1))
    probs = jnp.exp(scores - totals[..., None])
    attn_heads = ein("hqk,khd->qhd", probs.astype(bf16), v).astype(bf16)
    attn_flat = attn_heads.reshape(length, cols)
    attn_rows = lax.all_to_all(attn_flat, "seq", split_axis=0, concat_axis=1, tiled=True)

    x_own32 = x_own.astype(f32)
    residual = x_own32 + mm(attn_rows, out_full)
    normed_mid = norm_rows(residual, gain_mid).astype(bf16)

    x_all = lax.all_gather(normed_mid, AXES, axis=0, tiled=True)
    logits_all = mm(x_all, router_full)
    w_all = route_weights(logits_all, routes_all)

    local = first_expert + jnp.arange(n_loc, dtype=jnp.int32)
    match = routes_all.reshape(n_dev, tok_rows, top_k)[:, None] == local[None, :, None, None]
    hit = jnp.any(match, axis=-1)
    w_hit = jnp.sum(jnp.where(match, w_all.reshape(n_dev, 1, tok_rows, top_k), 0.0), axis=-1)
    tri = (jnp.arange(tok_rows)[:, None] <= jnp.arange(tok_rows)[None, :]).astype(bf16)
    place = ein("bet,tu->beu", hit.astype(bf16), tri).astype(jnp.int32) - 1
    slots = jnp.arange(capacity, dtype=jnp.int32)
    pick = hit[:, :, None, :] & (place[:, :, None, :] == slots[None, None, :, None])
    one = pick.astype(bf16)
    w_slot = jnp.sum(jnp.where(pick, w_hit[:, :, None, :], 0.0), axis=-1)
    rows_of = lambda a: ein("best,btd->ebsd", one, a.reshape(n_dev, tok_rows, width)).reshape(
        n_loc, n_dev * capacity, width
    )
    rows_in = rows_of(x_all).astype(bf16)
    rows_cot = rows_of(cot_all)
    w_rows = w_slot.transpose(1, 0, 2).reshape(n_loc, n_dev * capacity, 1)
    rows_grad = (w_rows * rows_cot).astype(bf16)
    gate = expert_gate.reshape(n_loc, per_loc, width, -1)
    up = expert_up.reshape(n_loc, per_loc, width, -1)
    down = expert_down.reshape(n_loc, per_loc, -1, width)

    pre_gate = ein("erd,epdf->eprf", rows_in, gate)
    pre_up = ein("erd,epdf->eprf", rows_in, up)
    sig = jax.nn.sigmoid(pre_gate)
    active = pre_gate * sig
    hidden = (active * pre_up).astype(bf16)
    hidden_grad = ein("erd,epfd->eprf", rows_grad, down)
    gate_grad = (hidden_grad * pre_up * sig * (1.0 + pre_gate * (1.0 - sig))).astype(bf16)
    up_grad = (hidden_grad * active).astype(bf16)
    back = ein("eprf,epdf->erd", gate_grad, gate) + ein("eprf,epdf->erd", up_grad, up)
    out = ein("eprf,epfd->erd", hidden, down)
    w_back = jnp.sum(rows_cot * out, axis=-1)
    spread = lambda a: ein(
        "best,ebsd->btd", one, a.astype(bf16).reshape(n_loc, n_dev, capacity, width)
    ).astype(bf16).reshape(n_dev * tok_rows, width)
    back_own = lax.psum_scatter(spread(back), AXES, scatter_dimension=0, tiled=True)
    w_tok = jnp.sum(
        jnp.where(pick, w_back.reshape(n_loc, n_dev, capacity).transpose(1, 0, 2)[..., None], 0.0), axis=2
    )
    w_parts = lax.all_to_all(w_tok, AXES, split_axis=0, concat_axis=0, tiled=True)
    w_by_expert = w_parts.reshape(experts, n_dev * n_loc // experts, tok_rows).sum(axis=1)
    own_match = (chosen[:, :, None] == jnp.arange(experts, dtype=jnp.int32)).astype(f32)
    weight_grad = jnp.sum(own_match * w_by_expert.T[:, None, :], axis=-1)
    moe_own = lax.psum_scatter(spread(w_rows * out), AXES, scatter_dimension=0, tiled=True)
    block_out = (residual + moe_own.astype(f32)).astype(bf16)

    down_grad = ein("eprf,erd->epfd", hidden, rows_grad).reshape(expert_down.shape)
    gate_weight_grad = ein("erd,eprf->epdf", rows_in, gate_grad).reshape(expert_gate.shape)
    up_weight_grad = ein("erd,eprf->epdf", rows_in, up_grad).reshape(expert_up.shape)

    logits = mm(normed_mid, router_full)
    _, route_back = jax.vjp(lambda values: route_weights(values, chosen), logits)
    logit_grad = route_back(weight_grad)[0].astype(bf16)
    normed_total = back_own.astype(f32) + mm_nt(logit_grad, router_full)
    logit_all = lax.all_gather(logit_grad, AXES, axis=0, tiled=True)
    x_cols = lax.dynamic_slice_in_dim(x_all, dev_at * shard, shard, 1)
    grad_router = mm_tn(x_cols, logit_all)
    cot32 = cot_own.astype(f32)
    _, norm_back = jax.vjp(norm_rows, residual, gain_mid)
    resid_part, gain_two = norm_back(normed_total)
    resid_grad = cot32 + resid_part
    resid_seq = lax.all_gather(resid_grad.astype(bf16), "seq", axis=0, tiled=True)

    grad_out_rows = mm_tn(attn_flat, resid_seq)
    grad_output = lax.psum_scatter(grad_out_rows, "fsdp", scatter_dimension=0, tiled=True)
    attn_grad = mm_nt(resid_seq, out_rows).astype(bf16).reshape(length, heads, HD)
    delta = jnp.sum(attn_grad.astype(f32) * attn_heads.astype(f32), axis=-1)
    v_grad = ein("hqk,qhd->khd", probs.astype(bf16), attn_grad).astype(bf16)
    p_grad = ein("qhd,khd->hqk", attn_grad, v)
    s_grad = (probs * (p_grad - delta.T[:, :, None]) * scale).astype(bf16)
    q_grad = ein("hqk,khd->qhd", s_grad, k).astype(bf16)
    k_grad = ein("hqk,qhd->khd", s_grad, q).astype(bf16)
    q_rows = rotate(q_grad.astype(f32), cosine, sine_tab, True).astype(bf16)
    k_rows = rotate(k_grad.astype(f32), cosine, sine_tab, True).astype(bf16)
    d_qkv = jnp.concatenate([a.reshape(length, cols) for a in (q_rows, k_rows, v_grad)], axis=1)
    in_part = mm_nt(d_qkv, w_qkv).astype(bf16)
    normed_in_grad = lax.psum_scatter(in_part, "seq", scatter_dimension=0, tiled=True).astype(f32)
    _, norm_back_in = jax.vjp(norm_rows, x_own32, gain_in)
    input_part, gain_one = norm_back_in(normed_in_grad)
    input_grad = resid_grad + input_part

    grad_qkv = mm_tn(normed_in, d_qkv).reshape(n_seq, n_fsdp, shard, 3 * cols)
    grad_qkv = lax.psum_scatter(grad_qkv, "fsdp", scatter_dimension=1, tiled=False)
    grad_qkv = lax.all_to_all(grad_qkv, "seq", split_axis=0, concat_axis=0, tiled=True)
    grad_qkv = grad_qkv.reshape(n_seq, shard, 3, cols).transpose(2, 1, 0, 3).reshape(3, shard, width)
    gains = lax.psum_scatter(
        jnp.stack([gain_one, gain_two]).reshape(2, n_dev, shard), AXES, scatter_dimension=1, tiled=False
    )
    return (
        block_out[None],
        input_grad[None],
        gains[0],
        grad_qkv[0],
        grad_qkv[1],
        grad_qkv[2],
        grad_output,
        gains[1],
        grad_router,
        gate_weight_grad,
        up_weight_grad,
        down_grad,
    )


def solution(mesh):
    rows3 = P("fsdp", "seq", None)
    flat = P(AXES)
    two = P(AXES, None)
    three = P(AXES, None, None)
    return jax.shard_map(
        body,
        mesh=mesh,
        in_specs=(rows3, rows3, rows3, flat, two, two, two, two, flat, two, three, three, three),
        out_specs=(rows3, rows3, flat, two, two, two, two, flat, two, three, three, three),
        check_vma=False,
    )
```

time: 2960 us -> 1340 us (0.45)
  waiting for transfers between devices: 1820 us -> 712 us
  blocking collectives: 488 us -> 201 us
  starting transfers between devices: 118 us -> 9.59 us
  local copies, waits for them, and re-layouts: 143 us -> 88.1 us
  other arithmetic: 93.1 us -> 40.5 us
    all_to_all x9 -> x2, waiting for transfers between devices: 1030 us -> 11 us  [the longest x1 11 us: body(): lax.all_to_all(w_tok, AXES, split_axis=0, concat_axis=0, tiled=True)]
    reduce_scatter x5, waiting for transfers between devices: 621 us -> 352 us  [the longest x1 167 us: body(): lax.psum_scatter(spread(back), AXES, scatter_dimension=0, tiled=True)]
    all_gather x1 -> x2, blocking collectives: 337 us -> 83.7 us  [the longest x1 42.9 us: body(): logit_all = lax.all_gather(logit_grad, AXES, axis=0, tiled=True)]
    all_gather x4 -> x6, waiting for transfers between devices: 166 us -> 347 us  [the longest x1 102 us: body(): x_all = lax.all_gather(normed_mid, AXES, axis=0, tiled=True)]
    all_to_all x9 -> x2, starting transfers between devices: 117 us -> 8.57 us  [the longest x1 5.73 us: body(): lax.all_to_all(grad_qkv, 'seq', split_axis=0, concat_axis=0, tiled=True)]
    unnamed x2 -> x1, blocking collectives: 97.8 us -> 45.8 us
    unnamed x143 -> x88, local copies, waits for them, and re-layouts: 5.17 us -> 51 us
    gather x7 -> x0, local copies, waits for them, and re-layouts: 36.6 us -> none  [the longest x1 14.7 us: body(): from_experts(piece_out)[target].reshape(tok_rows, top_k, model_width)]
  transfers between devices with their start and end apart: 18 -> 13, of which waited for: 15 -> 12; matrix products, arithmetic and copies ran while one was open for 13% -> 14% of each run, Pallas kernels for 0% -> 0%
where the time goes in v1:
time: 1340 us; the launch traced here: 1330 us
  waiting for transfers between devices  712 us (53%)
  matrix products  265 us (20%)
  blocking collectives  201 us (15%)
  local copies, waits for them, and re-layouts  88.1 us (7%)
  other arithmetic  40.5 us (3%)
  between operations  14.8 us (1%)
    dot_general x19, matrix products, ein(): return jnp.einsum(spec, *args, preferred_element_type=f32)  206 us
    reduce_scatter x1, waiting for transfers between devices, body(): lax.psum_scatter(spread(back), AXES, scatter_dimension=0, tiled=True)  167 us
    reduce_scatter x1, waiting for transfers between devices, body(): lax.psum_scatter(spread(w_rows * out), AXES, scatter_dimension=0, tiled=T...  139 us
    all_gather x1, waiting for transfers between devices, body(): x_all = lax.all_gather(normed_mid, AXES, axis=0, tiled=True)  102 us
    all_gather x1, waiting for transfers between devices, body(): lax.all_gather(resid_grad.astype(bf16), 'seq', axis=0, tiled=True)  73.9 us
    all_gather x1, waiting for transfers between devices, body(): x_seq = lax.all_gather(x_own, 'seq', axis=0, tiled=True)  69.8 us
    all_gather x1, waiting for transfers between devices, body(): cot_all = lax.all_gather(cot_own, AXES, axis=0, tiled=True)  68.4 us
    unnamed x88, local copies, waits for them, and re-layouts  51 us
  transfers between devices with their start and end apart: 13, of which 12 were waited for; matrix products, arithmetic and copies ran while one was open for 14% of the time, Pallas kernels for 0%

profile of v1, /device:TPU:0, one launch (start us, length us, event | category | flops | bytes accessed | tf_op | source)
XLA Modules:
  0.0 1330.9 jit_solution(16863959521056442889)
XLA Ops:
  12.9 30.4 %all_to_all.34 = bf16[8,64,896]{2,1,0:T(8,128)(2,1)S(1)} all-to-all(bf16[8,64,896]{2,1,0:T(8,128)(2,1)S(1)} %copy.233), channel_id=1, replica_groups=mesh['seq'=8,'fsdp'=4] {'seq'}, dimensions={0} | all-to-all | bytes 1835008 | tf_op jit(solution)/shard_map/all_to_all | solution.py:123
  50.0 25.2 %all-gather.19.cloned.1.call-done = bf16[8,256,896]{2,0,1:T(8,128)(2,1)} async-done(((bf16[8,64,896]{2,0,1:T(8,128)(2,1)}), bf16[8,256,896]{2,0,1:T(8,128)(2,1)}) %all-gather.19.cloned.1.call-update) | async-done | bytes 3670032 | tf_op jit(solution)/shard_map/all_gather | solution.py:124
  80.2 69.8 %all-gather.17.cloned.1.call-done = bf16[1,1024,2048]{2,1,0:T(8,128)(2,1)} async-done(((bf16[1,128,2048]{2,1,0:T(8,128)(2,1)}), bf16[1,1024,2048]{2,1,0:T(8,128)(2,1)}) %all-gather.17.cloned.1.call-update) | async-done | bytes 4194320 | tf_op jit(solution)/shard_map/all_gather | solution.py:104
  189.1 41.3 %all_to_all.35 = bf16[8,128,256]{1,2,0:T(8,128)(2,1)S(1)} all-to-all(bf16[8,128,256]{1,2,0:T(8,128)(2,1)S(1)} %copy.241), channel_id=1, replica_groups=mesh['seq'=8,'fsdp'=4] {'seq'}, dimensions={0} | all-to-all | bytes 1048576 | tf_op jit(solution)/shard_map/all_to_all | solution.py:145
  244.7 40.9 %all-gather.2 = s32[1,4096,8]{1,2,0:T(8,128)S(1)} all-gather(s32[1,128,8]{1,2,0:T(8,128)S(1)} %copy-done.24), channel_id=4, replica_groups=mesh['seq'=8,'fsdp'=4] {'seq','fsdp'}, dimensions={1}, use_global_device_ids=true | all-gather | bytes 135168 | tf_op jit(solution)/shard_map/all_gather | solution.py:103
  285.9 68.4 %all-gather.21.cloned.1.call-done = bf16[1,4096,2048]{2,1,0:T(8,128)(2,1)} async-done(((bf16[1,128,2048]{2,1,0:T(8,128)(2,1)}), bf16[1,4096,2048]{2,1,0:T(8,128)(2,1)}) %all-gather.21.cloned.1.call-update) | async-done | bytes 16777232 | tf_op jit(solution)/shard_map/all_gather | solution.py:131
  367.6 102.1 %all-gather.13.cloned.1.call-done = bf16[4096,2048]{1,0:T(8,128)(2,1)} async-done(((bf16[128,2048]{1,0:T(8,128)(2,1)}), bf16[4096,2048]{1,0:T(8,128)(2,1)}) %all-gather.13.cloned.1.call-update) | async-done | bytes 16777232 | tf_op jit(solution)/shard_map/all_gather | solution.py:151
  518.0 19.9 %fusion.3 = (f32[2,1024]{1,0:T(2,128)S(1)}, f32[2,1024,2048,1]{2,1,3,0:T(8,128)}) fusion(f32[2,32,32,2048]{3,2,1,0:T(8,128)} %copy.247, bf16[2,2,1024,512]{3,2,1,0:T(8,128)(2,1)S(1)} %get-tuple-element.133, bf16[2,2,512,2048]{3,2,1,0:T(8,128)(2,1)} %bitcast.295), kind=kOutput, calls=%fused_computation.8 | convolution fusion | flops 8598321152 | bytes 46145536 | tf_op jit(solution)/shard_map/eprf,epfd->erd/dot_general | solution.py:63
  552.2 17.0 %fusion.2 = (bf16[2,1024,2048]{2,1,0:T(8,128)(2,1)}, bf16[2,1024,2048]{2,1,0:T(8,128)(2,1)}) fusion(f32[2,32,32,2048]{3,2,1,0:T(8,128)} %copy.247, f32[2,1024]{1,0:T(2,128)S(1)} %mul.567, f32[2,1024,2048,1]{2,1,3,0:T(8,128)} %get-tuple-element.136), kind=kLoop, calls=%fused_computation.7 | loop fusion | flops 16777216 | bytes 50339840 | tf_op jit(solution)/shard_map/convert_element_type | solution.py:171
  569.1 18.9 %fusion.16 = (bf16[2,2,1024,512]{3,2,1,0:T(8,128)(2,1)}, bf16[2,2,1024,512]{3,2,1,0:T(8,128)(2,1)S(1)}) fusion(f32[2,1024,2,512]{3,1,2,0:T(8,128)} %fusion.98, f32[2,1024,2,512]{3,1,2,0:T(8,128)} %get-tuple-element.134, bf16[2,2,512,2048]{3,2,1,0:T(8,128)(2,1)} %bitcast.296, bf16[2,1024,2048]{2,1,0:T(8,128)(2,1)} %get-tuple-element.122), kind=kOutput, calls=%fused_computation.29 | convolution fusion | flops 8617197568 | bytes 41943040 | tf_op jit(solution)/shard_map/erd,epfd->eprf/dot_general | solution.py:63
  588.0 16.2 %fusion.99 = f32[2,1024,2048,1]{2,1,3,0:T(8,128)} fusion(bf16[2,2,1024,512]{3,2,1,0:T(8,128)(2,1)S(1)} %get-tuple-element.98, bf16[2,2,2048,512]{3,2,1,0:T(8,128)(2,1)} %bitcast.298), kind=kOutput, calls=%fused_computation.182 | convolution fusion | flops 8589934592 | bytes 29360128 | tf_op jit(solution)/shard_map/eprf,epdf->erd/dot_general | solution.py:63
  604.2 16.9 %fusion.1 = bf16[2,1024,2048]{2,1,0:T(8,128)(2,1)} fusion(f32[2,1024,2048,1]{2,1,3,0:T(8,128)} %fusion.99, bf16[2,2,1024,512]{3,2,1,0:T(8,128)(2,1)} %get-tuple-element.97, bf16[2,2,2048,512]{3,2,1,0:T(8,128)(2,1)} %bitcast.300), kind=kOutput, calls=%fused_computation.4 | convolution fusion | flops 8598323200 | bytes 37748736 | tf_op jit(solution)/shard_map/eprf,epdf->erd/dot_general | solution.py:63
  648.4 166.7 %reduce-scatter.8.cloned.1.call-done = bf16[128,2048]{1,0:T(8,128)(2,1)} async-done(((bf16[4096,2048]{1,0:T(8,128)(2,1)}), bf16[128,2048]{1,0:T(8,128)(2,1)}) %reduce-scatter.8.cloned.1.call-update) | async-done | bytes 524304 | tf_op jit(solution)/shard_map/reduce_scatter | solution.py:190
  818.4 73.9 %all-gather.15.cloned.1.call-done = bf16[1024,2048]{1,0:T(8,128)(2,1)} async-done(((bf16[128,2048]{1,0:T(8,128)(2,1)}), bf16[1024,2048]{1,0:T(8,128)(2,1)}) %all-gather.15.cloned.1.call-update) | async-done | bytes 4194320 | tf_op jit(solution)/shard_map/all_gather | solution.py:216
  943.0 16.9 %fusion.101 = f32[2,2,512,2048]{3,2,1,0:T(8,128)} fusion(bf16[2,2,1024,512]{3,2,1,0:T(8,128)(2,1)} %copy-done.34, bf16[2,1024,2048,1]{2,1,3,0:T(8,128)(2,1)} %bitcast.249), kind=kOutput, calls=%fused_computation.184 | convolution fusion | flops 8589934592 | bytes 29360128 | tf_op jit(solution)/shard_map/erd,eprf->epdf/dot_general | solution.py:63
  962.6 16.5 %fusion.102 = f32[2,2,512,2048]{3,2,1,0:T(8,128)} fusion(bf16[2,2,1024,512]{3,2,1,0:T(8,128)(2,1)} %get-tuple-element.97, bf16[2,1024,2048,1]{2,1,3,0:T(8,128)(2,1)} %bitcast.250), kind=kOutput, calls=%fused_computation.185 | convolution fusion | flops 8589934592 | bytes 29360128 | tf_op jit(solution)/shard_map/erd,eprf->epdf/dot_general | solution.py:63
  985.7 16.6 %fusion.9 = f32[2,2,512,2048]{3,2,1,0:T(8,128)} fusion(bf16[2,2,1024,512]{3,2,1,0:T(8,128)(2,1)} %copy-done.33, bf16[2,1024,2048]{2,1,0:T(8,128)(2,1)} %get-tuple-element.122), kind=kOutput, calls=%fused_computation.20 | convolution fusion | flops 8589934592 | bytes 29360128 | tf_op jit(solution)/shard_map/eprf,erd->epfd/dot_general | solution.py:63
  1002.3 16.4 %copy.269 = f32[4,2048,512]{2,1,0:T(8,128)} copy(f32[4,2048,512]{1,2,0:T(8,128)} %bitcast.240) | data formatting | bytes 33554432
  1018.6 16.5 %copy.270 = f32[4,2048,512]{2,1,0:T(8,128)} copy(f32[4,2048,512]{1,2,0:T(8,128)} %bitcast.241) | data formatting | bytes 33554432
  1035.1 42.9 %all_gather.35 = bf16[4096,64]{0,1:T(8,128)(2,1)S(1)} all-gather(bf16[128,64]{0,1:T(8,128)(2,1)S(1)} %multiply_convert_fusion.2), channel_id=1, replica_groups=mesh['seq'=8,'fsdp'=4] {'seq','fsdp'}, dimensions={0}, use_global_device_ids=true | all-gather | bytes 540672 | tf_op jit(solution)/shard_map/all_gather | solution.py:209
  1080.6 21.2 %reduce-scatter.10.cloned.1.call-done = bf16[128,2048]{1,0:T(8,128)(2,1)} async-done(((bf16[1024,2048]{1,0:T(8,128)(2,1)}), bf16[128,2048]{1,0:T(8,128)(2,1)}) %reduce-scatter.10.cloned.1.call-update) | async-done | bytes 524304 | tf_op jit(solution)/shard_map/reduce_scatter | solution.py:231
  1103.6 45.8 %all-reduce = f32[2,32,64]{2,0,1:T(2,128)S(1)} all-reduce(f32[2,32,64]{2,0,1:T(2,128)S(1)} %pad_maximum_fusion.7), channel_id=9, replica_groups=mesh['seq'=8,'fsdp'=4] {'seq','fsdp'}, use_global_device_ids=true, to_apply=%region_27.28.clone | all-reduce | flops 4096 | bytes 32768
  1150.0 138.5 %reduce-scatter.6.cloned.1.call-done = bf16[128,2048]{1,0:T(8,128)(2,1)} async-done(((bf16[4096,2048]{1,0:T(8,128)(2,1)}), bf16[128,2048]{1,0:T(8,128)(2,1)}) %reduce-scatter.6.cloned.1.call-update) | async-done | bytes 524304 | tf_op jit(solution)/shard_map/reduce_scatter | solution.py:198
  1299.3 25.0 %reduce-scatter.14.cloned.1.call-done = f32[64,2048]{1,0:T(8,128)} async-done(((f32[256,2048]{1,0:T(8,128)}), f32[64,2048]{1,0:T(8,128)}) %reduce-scatter.14.cloned.1.call-update) | async-done | bytes 524304 | tf_op jit(solution)/shard_map/reduce_scatter | solution.py:219
  (208 shorter events, 252.5 us)
Async XLA Ops:
  7.2 67.9 %all-gather.19.cloned.1.call-start = ((), (), s32[]{:S(2)}) async-start(), calls=%async_computation.18 | async-start | bytes 4587520 | tf_op jit(solution)/shard_map/all_gather | solution.py:124
  44.7 105.3 %all-gather.17.cloned.1.call-start = ((), (), s32[]{:S(2)}) async-start(), calls=%async_computation.17 | async-start | bytes 4718592 | tf_op jit(solution)/shard_map/all_gather | solution.py:104
  45.5 192.4 %all-gather.11.cloned.1.call-start = ((), (), s32[]{:S(2)}) async-start(), calls=%async_computation.9 | async-start | bytes 8650752 | tf_op jit(solution)/shard_map/all_gather | solution.py:129
  46.2 308.1 %all-gather.21.cloned.1.call-start = ((), (), s32[]{:S(2)}) async-start(), calls=%async_computation.19 | async-start | bytes 17301504 | tf_op jit(solution)/shard_map/all_gather | solution.py:131
  46.8 422.8 %all-gather.13.cloned.1.call-start = ((), (), s32[]{:S(2)}) async-start(), calls=%async_computation.10 | async-start | bytes 17301504 | tf_op jit(solution)/shard_map/all_gather | solution.py:151
  49.9 121.3 %copy-start.6 = (f32[1024,64]{1,0:T(8,128)}, f32[1024,64]{1,0:T(8,128)S(1)}, u32[]{:S(2)}) copy-start(f32[1024,64]{1,0:T(8,128)S(1)} %get-tuple-element.126) | copy-start | bytes 786436
  80.2 72.9 %copy-start.22 = (f32[2048]{0:T(1024)}, f32[2048]{0:T(1024)S(1)}, u32[]{:S(2)}) copy-start(f32[2048]{0:T(1024)S(1)} %get-tuple-element.85) | copy-start | bytes 24580
  80.2 162.5 %copy-start.20 = (f32[2048]{0:T(1024)}, f32[2048]{0:T(1024)S(1)}, u32[]{:S(2)}) copy-start(f32[2048]{0:T(1024)S(1)} %get-tuple-element.84) | copy-start | bytes 24580
  184.0 53.9 %copy-start.2 = (bf16[1,128,2048]{2,1,0:T(8,128)(2,1)S(1)}, bf16[1,128,2048]{2,1,0:T(8,128)(2,1)}, u32[]{:S(2)}) copy-start(bf16[1,128,2048]{2,1,0:T(8,128)(2,1)} %param.13) | copy-start | bytes 1572868
  242.7 42.9 %copy-start.30 = (f32[128]{0:T(128)}, f32[128]{0:T(128)S(1)}, u32[]{:S(2)}) copy-start(f32[128]{0:T(128)S(1)} %get-tuple-element.129) | copy-start | bytes 1540
  244.6 570.5 %reduce-scatter.8.cloned.1.call-start = ((), (), s32[]{:S(2)}) async-start(), calls=%async_computation.12 | async-start | bytes 17301504 | tf_op jit(solution)/shard_map/reduce_scatter | solution.py:190
  631.9 183.2 %copy-start.1 = (f32[128,2048]{1,0:T(8,128)S(1)}, f32[128,2048]{1,0:T(8,128)}, u32[]{:S(2)}) copy-start(f32[128,2048]{1,0:T(8,128)} %copy-done) | copy-start | bytes 3145732
  631.9 183.2 %copy-start.21 = (f32[2048]{0:T(1024)S(1)}, f32[2048]{0:T(1024)}, u32[]{:S(2)}) copy-start(f32[2048]{0:T(1024)} %copy-done.20) | copy-start | bytes 24580
  631.9 183.2 %copy-start.27 = (f32[128]{0:T(128)S(1)}, f32[128]{0:T(128)}, u32[]{:S(2)}) copy-start(f32[128]{0:T(128)} %copy-done.26) | copy-start | bytes 1540
  631.9 185.0 %copy-start.31 = (f32[128]{0:T(128)S(1)}, f32[128]{0:T(128)}, u32[]{:S(2)}) copy-start(f32[128]{0:T(128)} %copy-done.30) | copy-start | bytes 1540
  631.9 185.0 %copy-start.9 = (bf16[1,128,2048]{2,1,0:T(8,128)(2,1)S(1)}, bf16[1,128,2048]{2,1,0:T(8,128)(2,1)}, u32[]{:S(2)}) copy-start(bf16[1,128,2048]{2,1,0:T(8,128)(2,1)} %param.14) | copy-start | bytes 1572868
  634.3 13.9 %all-to-all-start.2 = ((f32[32,2,128]{2,1,0:T(2,128)}), f32[32,2,128]{2,1,0:T(2,128)S(1)}, u32[]{:S(2)}, u32[]{:S(2)}) async-start(f32[32,2,128]{2,1,0:T(2,128)} %get-tuple-element.92), calls=%async_computation.4 | async-start | bytes 65536 | tf_op jit(solution)/shard_map/all_to_all | solution.py:194
  637.2 255.1 %all-gather.15.cloned.1.call-start = ((), (), s32[]{:S(2)}) async-start(), calls=%async_computation.13 | async-start | bytes 4718592 | tf_op jit(solution)/shard_map/all_gather | solution.py:216
  818.1 161.8 %reduce-scatter.12.cloned.1.call-start = ((), (), s32[]{:S(2)}) async-start(), calls=%async_computation.15 | async-start | bytes 7864320 | tf_op jit(solution)/shard_map/reduce_scatter | solution.py:237
  818.4 83.8 %copy-start.11 = (bf16[1024,256]{0,1:T(8,128)(2,1)S(1)}, bf16[1024,256]{0,1:T(8,128)(2,1)}, u32[]{:S(2)}) copy-start(bf16[1024,256]{0,1:T(8,128)(2,1)} %copy-done.10) | copy-start | bytes 1572868
  922.4 179.5 %reduce-scatter.10.cloned.1.call-start = ((), (), s32[]{:S(2)}) async-start(), calls=%async_computation.14 | async-start | bytes 4718592 | tf_op jit(solution)/shard_map/reduce_scatter | solution.py:231
  930.5 358.0 %reduce-scatter.6.cloned.1.call-start = ((), (), s32[]{:S(2)}) async-start(), calls=%async_computation.11 | async-start | bytes 17301504 | tf_op jit(solution)/shard_map/reduce_scatter | solution.py:198
  941.6 382.6 %reduce-scatter.14.cloned.1.call-start = ((), (), s32[]{:S(2)}) async-start(), calls=%async_computation.16 | async-start | bytes 2621440 | tf_op jit(solution)/shard_map/reduce_scatter | solution.py:219
  979.9 311.4 %all-to-all-start.3 = ((f32[8,64,768]{2,1,0:T(8,128)}), f32[8,64,768]{2,1,0:T(8,128)}, u32[]{:S(2)}, u32[]{:S(2)}) async-start(f32[8,64,768]{2,1,0:T(8,128)} %bitcast.270), calls=%async_computation.7 | async-start | bytes 3145728 | tf_op jit(solution)/shard_map/all_to_all | solution.py:238
  (26 other events, 230.6 us)
Sparse Core Ops, SparseCore 0:
  44.9 30.1 all-gather.18
  77.2 72.7 all-gather.16
  152.9 84.9 all-gather.10
  240.6 113.6 all-gather.20
  357.0 112.5 all-gather.12
  632.1 182.9 reduce-scatter.7
  818.2 73.9 all-gather.14
  922.5 57.3 reduce-scatter.11
  983.6 118.2 reduce-scatter.9
  1104.0 184.4 reduce-scatter.5
  1291.6 32.5 reduce-scatter.13
